TPU v7x, 1024 devices: a whole 4x8x16 slice. The times are simulated.
1024 devices in a mesh: dp: 64 (over z, x_lo, core), tensor: 16 (over y, x_hi).
Axes of the slice: x: 4 (x_hi: 2, x_lo: 2; x = x_hi * 2 + x_lo), y: 8, z: 16, core: 2. Of those that a mesh axis runs over, the one named last changes fastest.
Arguments:
- tokens: bfloat16 [32768, 2048], P(('dp', 'tensor')), may hold values from -24 to 24
- gate_weight: bfloat16 [2048, 8192], P(None, 'tensor'), may hold values from -0.125 to 0.125
- up_act: bfloat16 [32768, 8192], P('dp', 'tensor'), may hold values from -6 to 6
- cotangent: bfloat16 [32768, 8192], P('dp', 'tensor'), may hold values from -6 to 6
- moment1: bfloat16 [2048, 8192], P('dp', 'tensor'), may hold values from -0.359375 to 0.359375
- moment2: bfloat16 [2048, 8192], P('dp', 'tensor'), may hold values from 0.0039978027 to 0.039794922
Outputs:
- in_grad: bfloat16 [32768, 2048], P(('dp', 'tensor'))
- up_grad: bfloat16 [32768, 8192], P('dp', 'tensor')
- new_moment1: bfloat16 [2048, 8192], P('dp', 'tensor')
- new_moment2: bfloat16 [2048, 8192], P('dp', 'tensor')
- update: float32 [2048, 8192], P('dp', 'tensor')
All inputs are finite; a program needn't handle non-finite values.
Results may differ from a plain program's by a relative error of at most 0.015.
Values may be sent and summed in bfloat16 or wider, within the bound.
A program may use at most 64 MiB of HBM per device.

v0:
```python
import math

import jax
import jax.numpy as jnp
from jax import lax
from jax.sharding import Mesh
from jax.sharding import PartitionSpec as P

DP = ("dp_0", "dp_1", "dp_2")
DP_TENSOR = ("dp_0", "dp_1", "dp_2", "tensor")


def sent_to_all(array, axis):
    copies = jnp.broadcast_to(array, (lax.axis_size(axis), *array.shape))
    return lax.all_to_all(copies, axis, split_axis=0, concat_axis=0, tiled=True)


def laid_out(parts, dim):
    lengths = list(parts.shape[1:])
    lengths[dim] *= parts.shape[0]
    return jnp.moveaxis(parts, 0, dim).reshape(lengths)


def collect(array, axis, dim):
    parts = sent_to_all(array, axis)
    return laid_out(parts, dim)


def split_up(array, dim, count):
    lengths = array.shape
    parts = array.reshape(*lengths[:dim], count, lengths[dim] // count, *lengths[dim + 1 :])
    return jnp.moveaxis(parts, dim, 0)


def sent_and_summed(array, axis, dim):
    count = lax.axis_size(axis)
    parts = lax.all_to_all(split_up(array, dim, count), axis, 0, 0, tiled=True)
    return jnp.sum(parts.astype(jnp.float32), axis=0)


def sum_in_order(parts, axes, order):
    lengths = [lax.axis_size(a) for a in axes]
    parts = parts.reshape(*lengths, *parts.shape[1:])
    parts = parts.transpose(*order, *range(len(axes), parts.ndim))
    parts = parts.reshape(-1, *parts.shape[len(axes) :])
    for k in order:
        parts = lax.psum_scatter(parts, axes[k], scatter_dimension=0, tiled=True)
    return parts[0]


def scatter_axes(array, axes, order, dim):
    count = lax.axis_size(axes)
    return sum_in_order(split_up(array, dim, count), axes, order)


def local(tokens, gate_weight, up_act, cotangent, moment1, moment2):
    gathered = collect(tokens, "tensor", 0)
    gate_pre = jnp.dot(gathered, gate_weight, preferred_element_type=jnp.float32)
    sigmoid_gate = jax.nn.sigmoid(gate_pre)
    cot_float = cotangent.astype(jnp.float32)
    up_grad = (cot_float * gate_pre * sigmoid_gate).astype(jnp.bfloat16)
    gate_grad = (
        cot_float
        * up_act.astype(jnp.float32)
        * sigmoid_gate
        * (1.0 + gate_pre * (1.0 - sigmoid_gate))
    ).astype(jnp.bfloat16)
    in_grad = sent_and_summed(
        lax.dot_general(
            gate_grad, gate_weight, (((1,), (1,)), ((), ())), preferred_element_type=jnp.float32
        ).astype(jnp.bfloat16),
        "tensor",
        0,
    ).astype(jnp.bfloat16)
    partial_value = lax.dot_general(
        gathered, gate_grad, (((0,), (0,)), ((), ())), preferred_element_type=jnp.float32
    ).astype(jnp.bfloat16)
    grad_shard = scatter_axes(partial_value.astype(jnp.float32), DP, (2, 0, 1), 0)
    grad_scale = 1.0 / math.sqrt(lax.axis_size(DP) * gathered.shape[0])
    grad = grad_shard * grad_scale
    first = 0.9 * moment1.astype(jnp.float32) + 0.1 * grad
    second = 0.95 * moment2.astype(jnp.float32) + 0.05 * grad * grad
    update = first / (jnp.sqrt(second) + 1e-08)
    return (in_grad, up_grad, first.astype(jnp.bfloat16), second.astype(jnp.bfloat16), update)


def solution(mesh):
    torus = Mesh(
        mesh.devices.reshape(16, 2, 2, mesh.shape["tensor"]), ("dp_0", "dp_1", "dp_2", "tensor")
    )
    in_specs = (
        P(DP_TENSOR, None),
        P(None, "tensor"),
        P(DP, "tensor"),
        P(DP, "tensor"),
        P(DP, "tensor"),
        P(DP, "tensor"),
    )
    out_specs = (
        P(DP_TENSOR, None),
        P(DP, "tensor"),
        P(DP, "tensor"),
        P(DP, "tensor"),
        P(DP, "tensor"),
    )
    return jax.shard_map(local, mesh=torus, in_specs=in_specs, out_specs=out_specs, check_vma=False)
```

profile of v0, /device:TPU:1, one launch (start us, length us, event | category | flops | bytes accessed | tf_op | source)
XLA Modules:
  0.0 228.7 jit_solution(14097402900745878388)
XLA Ops:
  7.2 0.0 copy-start
  7.2 0.0 reduce-scatter.4.cloned.1.call-start
  7.2 1.3 broadcast_in_dim.3
  8.5 0.0 copy-start.3
  8.5 0.0 copy-start.4
  8.5 54.9 %all_to_all.10 = bf16[16,32,2048]{2,1,0:T(8,128)(2,1)S(1)} all-to-all(bf16[16,32,2048]{2,1,0:T(8,128)(2,1)S(1)} %broadcast_in_dim.3), channel_id=1, replica_groups=mesh['dp_0'=16,'dp_1'=2,'dp_2'=2,'tensor'=16] {'tensor'}, dimensions={0} | all-to-all | bytes 4194304 | tf_op jit(solution)/shard_map/all_to_all | solution.py:15
  63.5 0.0 copy-done
  63.5 0.0 copy-done.3
  63.5 0.0 copy-done.4
  63.5 2.5 %fusion.4 = (bf16[512,512]{1,0:T(8,128)(2,1)}, bf16[512,512]{1,0:T(8,128)(2,1)S(1)}) fusion(bf16[512,512]{1,0:T(8,128)(2,1)S(1)} %copy-done.3, bf16[512,512]{1,0:T(8,128)(2,1)S(1)} %copy-done.4, bf16[512,2048]{1,0:T(8,128)(2,1)S(1)} %bitcast.28, bf16[2048,512]{1,0:T(8,128)(2,1)S(1)} %copy-done), kind=kOutput, calls=%fused_computation.9 | convolution fusion | flops 1077673984 | bytes 6291456 | tf_op jit(solution)/shard_map/dot_general | solution.py:58
  65.9 3.3 %convert_bitcast_fusion = f32[2048,512]{0,1:T(8,128)} fusion(bf16[512,512]{1,0:T(8,128)(2,1)S(1)} %get-tuple-element.6, bf16[512,2048]{1,0:T(8,128)(2,1)S(1)} %bitcast.29), kind=kOutput, calls=%fused_computation | convolution fusion | flops 1075838976 | bytes 6815744 | tf_op jit(solution)/shard_map/dot_general | solution.py:75
  69.2 5.4 %copy.13 = f32[2048,512]{1,0:T(8,128)} copy(f32[2048,512]{0,1:T(8,128)} %convert_bitcast_fusion) | data formatting | bytes 8388608 | tf_op jit(solution)/shard_map/reshape | solution.py:45
  74.6 5.0 %copy.14 = f32[2,16,2,32,512]{4,3,2,1,0:T(8,128)} copy(f32[2,16,2,32,512]{4,3,0,2,1:T(8,128)} %bitcast.27) | data formatting | bytes 8388608 | tf_op jit(solution)/shard_map/reshape | solution.py:45
  79.5 0.0 reduce-scatter.4.cloned.1.call-update
  79.6 0.0 reduce-scatter.6.cloned.1.call-start
  79.6 37.1 %reduce-scatter.4.cloned.1.call-done = f32[32,32,512]{2,1,0:T(8,128)} async-done(((f32[64,32,512]{2,1,0:T(8,128)}), f32[32,32,512]{2,1,0:T(8,128)}) %reduce-scatter.4.cloned.1.call-update) | async-done | bytes 2097168 | tf_op jit(solution)/shard_map/reduce_scatter | solution.py:47
  116.7 0.0 reduce-scatter.6.cloned.1.call-update
  116.7 2.6 %convolution_convert_fusion.1 = bf16[512,2048]{1,0:T(8,128)(2,1)} fusion(bf16[512,512]{1,0:T(8,128)(2,1)S(1)} %get-tuple-element.6, bf16[2048,512]{1,0:T(8,128)(2,1)S(1)} %copy-done), kind=kOutput, calls=%fused_computation.2 | convolution fusion | flops 1074790400 | bytes 4718592 | tf_op jit(solution)/shard_map/dot_general | solution.py:69
  119.3 7.0 %all-to-all-start.1 = ((bf16[16,32,2048]{2,1,0:T(8,128)(2,1)}), bf16[16,32,2048]{2,1,0:T(8,128)(2,1)}, u32[]{:S(2)}, u32[]{:S(2)}) async-start(bf16[16,32,2048]{2,1,0:T(8,128)(2,1)} %bitcast.30), calls=%async_computation.1 | async-start | bytes 4194304 | tf_op jit(solution)/shard_map/all_to_all | solution.py:37
  126.4 0.0 copy-start.1
  126.4 0.0 copy-start.2
  126.4 0.0 reduce-scatter.8.cloned.1.call-start
  126.5 62.2 %reduce-scatter.6.cloned.1.call-done = f32[2,32,512]{2,1,0:T(8,128)} async-done(((f32[32,32,512]{2,1,0:T(8,128)}), f32[2,32,512]{2,1,0:T(8,128)}) %reduce-scatter.6.cloned.1.call-update) | async-done | bytes 131088 | tf_op jit(solution)/shard_map/reduce_scatter | solution.py:47
  188.7 0.0 reduce-scatter.8.cloned.1.call-update
  188.7 0.0 all-to-all-done.1
  188.7 2.7 %reduce_sum.12 = bf16[32,2048]{1,0:T(8,128)(2,1)} reduce(bf16[16,32,2048]{2,1,0:T(8,128)(2,1)} %all-to-all-done.1, bf16[]{:T(256)} %constant.4.clone.1), dimensions={0}, to_apply=%region_0.0 | reduce | flops 983040 | bytes 2228226 | tf_op jit(solution)/shard_map/reduce_sum | solution.py:38
  191.4 29.2 %reduce-scatter.8.cloned.1.call-done = f32[1,32,512]{2,1,0:T(8,128)} async-done(((f32[2,32,512]{2,1,0:T(8,128)}), f32[1,32,512]{2,1,0:T(8,128)}) %reduce-scatter.8.cloned.1.call-update) | async-done | bytes 65552 | tf_op jit(solution)/shard_map/reduce_scatter | solution.py:47
  220.6 0.0 copy-done.1
  220.6 0.0 copy-done.2
  220.6 1.5 add_divide_fusion.1
Async XLA Ops:
  7.2 56.3 %copy-start = (bf16[2048,512]{1,0:T(8,128)(2,1)S(1)}, bf16[2048,512]{1,0:T(8,128)(2,1)}, u32[]{:S(2)}) copy-start(bf16[2048,512]{1,0:T(8,128)(2,1)} %param.7) | copy-start | bytes 6291460
  7.2 109.5 %reduce-scatter.4.cloned.1.call-start = ((), (), s32[]{:S(2)}) async-start(), calls=%async_computation.5 | async-start | bytes 6291456 | tf_op jit(solution)/shard_map/reduce_scatter | solution.py:47
  8.5 55.0 %copy-start.3 = (bf16[512,512]{1,0:T(8,128)(2,1)S(1)}, bf16[512,512]{1,0:T(8,128)(2,1)}, u32[]{:S(2)}) copy-start(bf16[512,512]{1,0:T(8,128)(2,1)} %param.9) | copy-start | bytes 1572868
  8.5 55.0 %copy-start.4 = (bf16[512,512]{1,0:T(8,128)(2,1)S(1)}, bf16[512,512]{1,0:T(8,128)(2,1)}, u32[]{:S(2)}) copy-start(bf16[512,512]{1,0:T(8,128)(2,1)} %param.8) | copy-start | bytes 1572868
  79.6 109.1 %reduce-scatter.6.cloned.1.call-start = ((), (), s32[]{:S(2)}) async-start(), calls=%async_computation.6 | async-start | bytes 2228224 | tf_op jit(solution)/shard_map/reduce_scatter | solution.py:47
  119.3 69.3 %all-to-all-start.1 = ((bf16[16,32,2048]{2,1,0:T(8,128)(2,1)}), bf16[16,32,2048]{2,1,0:T(8,128)(2,1)}, u32[]{:S(2)}, u32[]{:S(2)}) async-start(bf16[16,32,2048]{2,1,0:T(8,128)(2,1)} %bitcast.30), calls=%async_computation.1 | async-start | bytes 4194304 | tf_op jit(solution)/shard_map/all_to_all | solution.py:37
  126.4 94.2 %copy-start.1 = (bf16[32,512]{1,0:T(8,128)(2,1)S(1)}, bf16[32,512]{1,0:T(8,128)(2,1)}, u32[]{:S(2)}) copy-start(bf16[32,512]{1,0:T(8,128)(2,1)} %param.10) | copy-start | bytes 98308
  126.4 94.2 %copy-start.2 = (bf16[32,512]{1,0:T(8,128)(2,1)S(1)}, bf16[32,512]{1,0:T(8,128)(2,1)}, u32[]{:S(2)}) copy-start(bf16[32,512]{1,0:T(8,128)(2,1)} %param.11) | copy-start | bytes 98308
  126.4 94.2 %reduce-scatter.8.cloned.1.call-start = ((), (), s32[]{:S(2)}) async-start(), calls=%async_computation.7 | async-start | bytes 196608 | tf_op jit(solution)/shard_map/reduce_scatter | solution.py:47
Sparse Core Ops, SparseCore 0:
  79.7 36.9 reduce-scatter.3
  120.1 68.4 reduce-scatter.5
  192.0 28.5 reduce-scatter.7
where the time goes:
time: 230 us; the launch traced here: 229 us
  waiting for transfers between devices  129 us (56%)
  blocking collectives  54.9 us (24%)
  between operations  13.8 us (6%)
  local copies, waits for them, and re-layouts  11.6 us (5%)
  matrix products  8.32 us (4%)
  starting transfers between devices  7.17 us (3%)
  other arithmetic  4.19 us (2%)
    reduce_scatter x3, waiting for transfers between devices, sum_in_order(): parts = lax.psum_scatter(parts, axes[k], scatter_dimension=0, tiled=True)  129 us
    all_to_all x1, blocking collectives, sent_to_all(): return lax.all_to_all(copies, axis, split_axis=0, concat_axis=0, tiled=True)  54.9 us
    reshape x2, local copies, waits for them, and re-layouts, sum_in_order(): parts = parts.reshape(-1, *parts.shape[len(axes):])  10.3 us
    all_to_all x1, starting transfers between devices, sent_and_summed(): parts = lax.all_to_all(split_up(array, dim, count), axis, 0, 0, tiled=True)  7.05 us
  transfers between devices with their start and end apart: 4, of which 3 were waited for; matrix products, arithmetic and copies ran while one was open for 2% of the time, Pallas kernels for 0%

commit v1 on v0

v1 whole, which is shorter than its diff:
```python
import math

import jax
import jax.numpy as jnp
from jax import lax
from jax.experimental import pallas as pl
from jax.experimental.pallas import tpu as pltpu
from jax.sharding import PartitionSpec as P

F32, BF16 = jnp.float32, jnp.bfloat16
Y, Z = 8, 16
BLK = 32


def slot(dy, c):
    if dy == 0:
        return c
    if dy == Y // 2:
        return 14 + c
    return (4 * dy if dy > 0 else -4 * dy - 2) + c


def kernel(
    tok_in, wgt_in, up_in, cot_in, m1_in, m2_in,
    ig_out, upg_out, m1_out, m2_out, upd_out,
    tok, wgt, up, cot, upg, gg, term, ir_r, ir_l, xh_s, xh_r,
    w, co_r, zs, zr_r, zr_l, xl_s, xl_r, m1, m2, ig, nm1, nm2, upd,
    ld_sem, up_sem, cot_sem, st_sem, upg_sem,
    g_ss, g_rs, x_ss, x_rs, co_ss, co_rs, z_ss, z_rs, i_ss, i_rs,
):
    d = lax.axis_index("dp")
    t = lax.axis_index("tensor")
    z, x_lo, core = d // 4, (d // 2) % 2, d % 2
    y, x_hi = t // 2, t % 2
    yr = (d, (t + 2) % 16)
    yl = (d, (t + 14) % 16)
    xh = (d, t + 1 - 2 * x_hi)
    zr = ((d + 4) % 64, t)
    zl = ((d + 60) % 64, t)
    xl = (d + 2 - 4 * x_lo, t)
    co = (d + 1 - 2 * core, t)

    def remote(src, dst, ss, rs, to):
        return pltpu.make_async_remote_copy(
            src_ref=src, dst_ref=dst, send_sem=ss, recv_sem=rs,
            device_id=to, device_id_type=pl.DeviceIdType.MESH,
        )

    def rows(s, half=None):
        if half is None:
            return pl.ds(BLK * s, BLK)
        return pl.ds(BLK * s + 16 * half, 16)

    def t_of(dy, c):
        return 2 * ((y + dy + Y) % Y) + (x_hi if c == 0 else 1 - x_hi)

    places = [(dy, c) for dy in (0, -1, 1, -2, 2, -3, 3, 4) for c in (0, 1)]

    ld_tok = pltpu.make_async_copy(tok_in, tok.at[rows(0)], ld_sem.at[0])
    ld_tok.start()
    ld_wgt = pltpu.make_async_copy(wgt_in, wgt, ld_sem.at[1])
    ld_wgt.start()
    loads = {}
    for dy, c in places:
        s = slot(dy, c)
        a = pltpu.make_async_copy(up_in.at[t_of(dy, c)], up.at[rows(s)], up_sem.at[s])
        b = pltpu.make_async_copy(cot_in.at[t_of(dy, c)], cot.at[rows(s)], cot_sem.at[s])
        a.start()
        b.start()
        loads[s] = (a, b)
    ld_m1 = pltpu.make_async_copy(m1_in, m1, ld_sem.at[2])
    ld_m2 = pltpu.make_async_copy(m2_in, m2, ld_sem.at[3])
    ld_m1.start()
    ld_m2.start()

    barrier = pltpu.get_barrier_semaphore()
    for peer in (yr, yl, xh, zr, zl, xl, co):
        pl.semaphore_signal(barrier, inc=1, device_id=peer, device_id_type=pl.DeviceIdType.MESH)
    pl.semaphore_wait(barrier, 7)

    g = {}
    for h in range(1, 5):
        for c in range(2):
            hr, hl = (0, 1) if h == 4 else (None, None)
            g[0, h, c] = remote(
                tok.at[rows(slot(1 - h, c), hr)],
                tok.at[rows(slot(-h if h < 4 else 4, c), hr)],
                g_ss.at[0, h - 1, c], g_rs.at[0, h - 1, c], yr,
            )
            g[1, h, c] = remote(
                tok.at[rows(slot(h - 1, c), hl)],
                tok.at[rows(slot(h, c), hl)],
                g_ss.at[1, h - 1, c], g_rs.at[1, h - 1, c], yl,
            )
    gx = remote(tok.at[rows(0)], tok.at[rows(1)], x_ss.at[0], x_rs.at[0], xh)

    upg_st = []

    def block(first, count):
        for s in range(first, first + count):
            loads[s][0].wait()
            loads[s][1].wait()
        r = pl.ds(BLK * first, BLK * count)
        gp = jnp.dot(tok[r, :], wgt[...], preferred_element_type=F32)
        sig = 1.0 / (1.0 + jnp.exp(-gp))
        cf = cot[r, :].astype(F32)
        upg[r, :] = (cf * gp * sig).astype(BF16)
        g16 = (cf * up[r, :].astype(F32) * sig * (1.0 + gp * (1.0 - sig))).astype(BF16)
        gg[r, :] = g16
        term[r, :] = lax.dot_general(
            g16, wgt[...], (((1,), (1,)), ((), ())), preferred_element_type=F32
        ).astype(BF16)
        for dy, c in places:
            s = slot(dy, c)
            if first <= s < first + count:
                cp = pltpu.make_async_copy(upg.at[rows(s)], upg_out.at[t_of(dy, c)], upg_sem.at[s])
                cp.start()
                upg_st.append(cp)

    ld_tok.wait()
    g[0, 1, 0].start()
    g[1, 1, 0].start()
    gx.start()
    gx.wait_recv()
    g[0, 1, 1].start()
    g[1, 1, 1].start()
    ld_wgt.wait()
    block(0, 2)
    for h in range(1, 4):
        for c in range(2):
            for side in range(2):
                g[side, h, c].wait_recv()
                g[side, h + 1, c].start()
        block(4 * h - 2, 4)
    for c in range(2):
        for side in range(2):
            g[side, 4, c].wait_recv()
    block(14, 2)

    ir = (ir_r, ir_l)
    i = {}
    for s in range(1, 5):
        for u in range(2):
            for side in range(2):
                half = side if s == 1 else None
                dy = 5 - s if side == 0 or s == 1 else s - 5
                dst = ir[side].at[s - 1, u]
                if half is not None:
                    dst = ir[side].at[s - 1, u, pl.ds(16 * half, 16)]
                i[side, s, u] = remote(
                    term.at[rows(slot(dy, u), half)], dst,
                    i_ss.at[side, s - 1, u], i_rs.at[side, s - 1, u], yr if side == 0 else yl,
                )
    ix = remote(xh_s, xh_r, x_ss.at[1], x_rs.at[1], xh)

    for u in (1, 0):
        for side in range(2):
            i[side, 1, u].start()

    def i_step(k):
        s, u = (k + 1) // 2, k % 2
        for side in range(2):
            i[side, s, u].wait_recv()
            if s == 4:
                continue
            dy = 4 - s if side == 0 else s - 4
            if s == 1:
                r = rows(slot(dy, u), side)
                got = ir[side][0, u, pl.ds(16 * side, 16), :]
            else:
                r = rows(slot(dy, u))
                got = ir[side][s - 1, u]
            term[r, :] = (term[r, :].astype(F32) + got.astype(F32)).astype(BF16)
            i[side, s + 1, u].start()
        if s == 4 and u == 1:
            xh_s[...] = (
                term[rows(1), :].astype(F32) + ir_r[3, 1].astype(F32) + ir_l[3, 1].astype(F32)
            ).astype(BF16)
            ix.start()

    cos = [
        remote(w.at[k, :, 1 - core], co_r.at[k], co_ss.at[k], co_rs.at[k], co) for k in range(Z)
    ]

    def w_part(dzs):
        for dz in dzs:
            k = dz % Z
            zt = (z + dz + Z) % Z
            cols = tok[:, pl.ds(pl.multiple_of(zt * 128, 128), 128)]
            part = lax.dot_general(
                cols, gg[...], (((0,), (0,)), ((), ())), preferred_element_type=F32
            )
            w[k] = part.astype(BF16).reshape(2, 2, BLK, part.shape[-1])
            cos[k].start()

    zrv = (zr_r, zr_l)
    zc = {}
    for s in range(1, 9):
        for side in range(2):
            for q in range(2):
                if s == 1 and q != side:
                    continue
                k = (9 - s if side == 0 else s - 9) % Z
                zc[side, s, q] = remote(
                    zs.at[k, q], zrv[side].at[s - 1, q],
                    z_ss.at[side, s - 1, q], z_rs.at[side, s - 1, q], zr if side == 0 else zl,
                )

    def own(k, q):
        return w[k, q, core].astype(F32) + co_r[k, q].astype(F32)

    def z_step(s):
        for side in range(2):
            cos[(8 - s if side == 0 else s - 8) % Z].wait_recv()
        for q in range(2):
            for side in range(2):
                k = (8 - s if side == 0 else s - 8) % Z
                val = own(k, q)
                if s > 1 or q == side:
                    zc[side, s, q].wait_recv()
                    val = val + zrv[side][s - 1, q].astype(F32)
                zs[k, q] = val.astype(BF16)
                zc[side, s + 1, q].start()

    w_part([8])
    w_part([7, -7])
    cos[8].wait_recv()
    for q in range(2):
        zs[8, q] = own(8, q).astype(BF16)
        zc[q, 1, q].start()
    w_part([6, -6])
    for k in range(1, 8):
        z_step(k)
        if k < 6:
            w_part([6 - k, k - 6])
        elif k == 6:
            w_part([0])
        i_step(k)

    cos[0].wait_recv()
    for q in range(2):
        for side in range(2):
            zc[side, 8, q].wait_recv()

    def total(q):
        return (
            w[0, q, core].astype(F32) + co_r[0, q].astype(F32)
            + zr_r[7, q].astype(F32) + zr_l[7, q].astype(F32)
        )

    xl_s[...] = total(1 - x_lo).astype(BF16)
    xc = remote(xl_s, xl_r, x_ss.at[2], x_rs.at[2], xl)
    xc.start()
    i_step(8)
    ld_m1.wait()
    ld_m2.wait()
    mine = total(x_lo)
    xc.wait_recv()
    grad = (mine + xl_r[...].astype(F32)) * (1.0 / math.sqrt(32768))
    first = 0.9 * m1[...].astype(F32) + 0.1 * grad
    second = 0.95 * m2[...].astype(F32) + 0.05 * grad * grad
    upd[...] = first / (jnp.sqrt(second) + 1e-8)
    nm1[...] = first.astype(BF16)
    nm2[...] = second.astype(BF16)
    stores = [
        pltpu.make_async_copy(upd, upd_out, st_sem.at[0]),
        pltpu.make_async_copy(nm1, m1_out, st_sem.at[1]),
        pltpu.make_async_copy(nm2, m2_out, st_sem.at[2]),
    ]
    for st in stores:
        st.start()
    ix.wait_recv()
    ig[...] = (
        term[rows(0), :].astype(F32) + ir_r[3, 0].astype(F32) + ir_l[3, 0].astype(F32)
        + xh_r[...].astype(F32)
    ).astype(BF16)
    stores.append(pltpu.make_async_copy(ig, ig_out, st_sem.at[3]))
    stores[-1].start()

    gx.wait_send()
    ix.wait_send()
    xc.wait_send()
    for cp in [*g.values(), *i.values(), *cos, *zc.values()]:
        cp.wait_send()
    for st in [*upg_st, *stores]:
        st.wait()


def local(tokens, gate_weight, up_act, cotangent, moment1, moment2):
    dw, hid = gate_weight.shape
    any_spec = pl.BlockSpec(memory_space=pl.ANY)
    vm = pltpu.VMEM
    dma = pltpu.SemaphoreType.DMA
    ig, upg, nm1, nm2, upd = pl.pallas_call(
        kernel,
        out_shape=(
            jax.ShapeDtypeStruct((BLK, dw), BF16),
            jax.ShapeDtypeStruct((16, BLK, hid), BF16),
            jax.ShapeDtypeStruct((BLK, hid), BF16),
            jax.ShapeDtypeStruct((BLK, hid), BF16),
            jax.ShapeDtypeStruct((BLK, hid), F32),
        ),
        in_specs=[any_spec] * 6,
        out_specs=(any_spec,) * 5,
        scratch_shapes=[
            vm((512, dw), BF16),
            vm((dw, hid), BF16),
            vm((512, hid), BF16),
            vm((512, hid), BF16),
            vm((512, hid), BF16),
            vm((512, hid), BF16),
            vm((512, dw), BF16),
            vm((4, 2, BLK, dw), BF16),
            vm((4, 2, BLK, dw), BF16),
            vm((BLK, dw), BF16),
            vm((BLK, dw), BF16),
            vm((Z, 2, 2, BLK, hid), BF16),
            vm((Z, 2, BLK, hid), BF16),
            vm((Z, 2, BLK, hid), BF16),
            vm((8, 2, BLK, hid), BF16),
            vm((8, 2, BLK, hid), BF16),
            vm((BLK, hid), BF16),
            vm((BLK, hid), BF16),
            vm((BLK, hid), BF16),
            vm((BLK, hid), BF16),
            vm((BLK, dw), BF16),
            vm((BLK, hid), BF16),
            vm((BLK, hid), BF16),
            vm((BLK, hid), F32),
            dma((4,)), dma((16,)), dma((16,)), dma((4,)), dma((16,)),
            dma((2, 4, 2)), dma((2, 4, 2)), dma((3,)), dma((3,)),
            dma((Z,)), dma((Z,)), dma((2, 8, 2)), dma((2, 8, 2)),
            dma((2, 4, 2)), dma((2, 4, 2)),
        ],
        compiler_params=pltpu.CompilerParams(collective_id=0, has_side_effects=True),
    )(
        tokens,
        gate_weight,
        up_act.reshape(16, BLK, hid),
        cotangent.reshape(16, BLK, hid),
        moment1,
        moment2,
    )
    return ig, upg.reshape(512, hid), nm1, nm2, upd


def solution(mesh):
    rows, cols, both = P(("dp", "tensor"), None), P(None, "tensor"), P("dp", "tensor")
    return jax.shard_map(
        local,
        mesh=mesh,
        in_specs=(rows, cols, both, both, both, both),
        out_specs=(rows, both, both, both, both),
        check_vma=False,
    )
```

time: 230 us -> 88.1 us (0.38)
  the two profiles are of different devices: /device:TPU:1 before, /device:TPU:24 now
where the time goes in v1:
time: 88.1 us; the launch traced here: 87.8 us
  Pallas kernels  79.5 us (90%)
  local copies, waits for them, and re-layouts  7.66 us (9%)
    pallas_call x1, Pallas kernels, local(): pl.pallas_call(kernel, out_shape=(jax.ShapeDtypeStruct((BLK, dw), BF16),...  79.5 us
    unnamed x5, local copies, waits for them, and re-layouts  7.66 us

profile of v1, /device:TPU:24, one launch (start us, length us, event | category | flops | bytes accessed | tf_op | source)
XLA Modules:
  0.0 87.8 jit_solution(14842533657421986368)
XLA Ops:
  0.6 79.5 %shard_map.101 = (bf16[32,2048]{1,0:T(8,128)(2,1)}, bf16[16,32,512]{2,1,0:T(8,128)(2,1)}, bf16[32,512]{1,0:T(8,128)(2,1)}, bf16[32,512]{1,0:T(8,128)(2,1)}, f32[32,512]{1,0:T(8,128)}) custom-call(bf16[32,2048]{1,0:T(8,128)(2,1)} %tok_in.1, bf16[2048,512]{1,0:T(8,128)(2,1)} %wgt_in.1, bf16[16,32,512]{2,1,0:T(8,128)(2,1)} %bitcast.3, ...), custom_call_target="tpu_custom_call" | custom-call | tf_op jit(solution)/shard_map/pallas_call | solution.py:294
  80.1 1.6 %copy.16 = bf16[32,2048]{1,0:T(8,128)(2,1)} copy(bf16[32,2048]{1,0:T(8,128)(2,1)} %get-tuple-element.20) | data formatting | bytes 262144
  81.7 1.9 %copy.17 = bf16[512,512]{1,0:T(8,128)(2,1)} copy(bf16[512,512]{1,0:T(8,128)(2,1)} %bitcast.5) | data formatting | bytes 1048576
  83.5 1.4 %copy.18 = bf16[32,512]{1,0:T(8,128)(2,1)} copy(bf16[32,512]{1,0:T(8,128)(2,1)} %get-tuple-element.22) | data formatting | bytes 65536
  84.9 1.4 %copy.19 = bf16[32,512]{1,0:T(8,128)(2,1)} copy(bf16[32,512]{1,0:T(8,128)(2,1)} %get-tuple-element.23) | data formatting | bytes 65536
  86.3 1.5 %copy.20 = f32[32,512]{1,0:T(8,128)} copy(f32[32,512]{1,0:T(8,128)} %get-tuple-element.24) | data formatting | bytes 131072

commit v2 on v1

v2 whole, which is shorter than its diff:
```python
import math

import jax
import jax.numpy as jnp
from jax import lax
from jax.experimental import pallas as pl
from jax.experimental.pallas import tpu as pltpu
from jax.sharding import PartitionSpec as P

F32, BF16 = jnp.float32, jnp.bfloat16
Y, Z = 8, 16
BLK = 32


def slot(dy, c):
    if dy == 0:
        return c
    if dy == Y // 2:
        return 14 + c
    return (4 * dy if dy > 0 else -4 * dy - 2) + c


def kernel(
    tok_in, wgt_in, up_in, cot_in,
    upg_out, ig, grad,
    tok, wgt, up, cot, upg, gg, term, ir_r, ir_l, xh_s, xh_r,
    w, co_r, zs, zr_r, zr_l, xl_s, xl_r,
    ld_sem, up_sem, cot_sem, upg_sem,
    g_ss, g_rs, gx_ss, gx_rs, x_ss, x_rs, co_ss, co_rs, z_ss, z_rs, i_ss, i_rs,
):
    d = lax.axis_index("dp")
    t = lax.axis_index("tensor")
    z, x_lo, core = d // 4, (d // 2) % 2, d % 2
    y, x_hi = t // 2, t % 2
    yn = ((d, (t + 2) % 16), (d, (t + 14) % 16))
    xh = (d, t + 1 - 2 * x_hi)
    zn = (((d + 4) % 64, t), ((d + 60) % 64, t))
    zn2 = (((d + 8) % 64, t), ((d + 56) % 64, t))
    xl = (d + 2 - 4 * x_lo, t)
    co = (d + 1 - 2 * core, t)

    def remote(src, dst, ss, rs, to):
        return pltpu.make_async_remote_copy(
            src_ref=src, dst_ref=dst, send_sem=ss, recv_sem=rs,
            device_id=to, device_id_type=pl.DeviceIdType.MESH,
        )

    def rows(s, half=None):
        if half is None:
            return pl.ds(BLK * s, BLK)
        return pl.ds(BLK * s + 16 * half, 16)

    def t_of(dy, c):
        return 2 * ((y + dy + Y) % Y) + (x_hi if c == 0 else 1 - x_hi)

    places = [(dy, c) for dy in (0, -1, 1, -2, 2, -3, 3, 4) for c in (0, 1)]

    ld_tok = pltpu.make_async_copy(tok_in, tok.at[rows(0)], ld_sem.at[0])
    ld_tok.start()
    ld_wgt = pltpu.make_async_copy(wgt_in, wgt, ld_sem.at[1])
    ld_wgt.start()
    loads = {}
    for dy, c in places:
        s = slot(dy, c)
        a = pltpu.make_async_copy(up_in.at[t_of(dy, c)], up.at[rows(s)], up_sem.at[s])
        b = pltpu.make_async_copy(cot_in.at[t_of(dy, c)], cot.at[rows(s)], cot_sem.at[s])
        a.start()
        b.start()
        loads[s] = (a, b)

    barrier = pltpu.get_barrier_semaphore()
    for peer in (*yn, xh, *zn, *zn2, xl, co):
        pl.semaphore_signal(barrier, inc=1, device_id=peer, device_id_type=pl.DeviceIdType.MESH)
    pl.semaphore_wait(barrier, 9)

    g = {}
    units = ((0, 1), (0, 0), (1, 0))
    for side in range(2):
        sg = -1 if side == 0 else 1
        for h in range(1, 5):
            for n, (c, half) in enumerate(units):
                if h == 4 and (n == 0) == (side == 0):
                    continue
                g[side, h, n] = remote(
                    tok.at[rows(slot(sg * (h - 1), c), half)],
                    tok.at[rows(slot(sg * h if h < 4 else 4, c), half)],
                    g_ss.at[side, h - 1, n], g_rs.at[side, h - 1, n], yn[side],
                )
    xa = remote(tok.at[rows(0, 0)], tok.at[rows(1, 0)], gx_ss.at[8], gx_rs.at[8], xh)
    xb = {
        dy: remote(
            tok.at[rows(slot(dy, 0), 1)], tok.at[rows(slot(dy, 1), 1)],
            gx_ss.at[dy + 3], gx_rs.at[dy + 3], xh,
        )
        for dy in (0, -1, 1, -2, 2, -3, 3, 4)
    }

    upg_st = []

    def gate(first, count):
        for s in range(first, first + count):
            loads[s][0].wait()
            loads[s][1].wait()
        r = pl.ds(BLK * first, BLK * count)
        gp = jnp.dot(tok[r, :], wgt[...], preferred_element_type=F32)
        sig = 1.0 / (1.0 + jnp.exp(-gp))
        cf = cot[r, :].astype(F32)
        upg[r, :] = (cf * gp * sig).astype(BF16)
        gg[r, :] = (cf * up[r, :].astype(F32) * sig * (1.0 + gp * (1.0 - sig))).astype(BF16)

    def terms(first, count):
        r = pl.ds(BLK * first, BLK * count)
        term[r, :] = lax.dot_general(
            gg[r, :], wgt[...], (((1,), (1,)), ((), ())), preferred_element_type=F32
        ).astype(BF16)
        for dy, c in places:
            s = slot(dy, c)
            if first <= s < first + count:
                cp = pltpu.make_async_copy(upg.at[rows(s)], upg_out.at[t_of(dy, c)], upg_sem.at[s])
                cp.start()
                upg_st.append(cp)

    ld_tok.wait()
    for n in range(2):
        for side in range(2):
            g[side, 1, n].start()
    xa.start()
    xb[0].start()
    xa.wait_recv()
    for side in range(2):
        g[side, 1, 2].start()
    ld_wgt.wait()
    for h in range(1, 4):
        for n in range(3):
            for side in range(2):
                g[side, h, n].wait_recv()
                if (side, h + 1, n) in g:
                    g[side, h + 1, n].start()
                if n == 0:
                    xb[-h if side == 0 else h].start()
            if n == 1 and h > 1:
                if h == 2:
                    xb[0].wait_recv()
                    gate(0, 2)
                    terms(0, 2)
                else:
                    xb[1 - h].wait_recv()
                    xb[h - 1].wait_recv()
                    gate(4 * h - 6, 4)
                    terms(4 * h - 6, 4)
        if h == 2:
            xb[-1].wait_recv()
            xb[1].wait_recv()
            gate(2, 4)
            terms(2, 4)
    g[1, 4, 0].wait_recv()
    xb[4].start()
    xb[-3].wait_recv()
    xb[3].wait_recv()
    gate(10, 4)
    terms(10, 4)
    g[0, 4, 1].wait_recv()
    g[0, 4, 2].wait_recv()
    xb[4].wait_recv()
    gate(14, 2)

    ir = (ir_r, ir_l)
    i = {}
    for s in range(1, 5):
        for u in range(2):
            for side in range(2):
                half = side if s == 1 else None
                dy = 5 - s if side == 0 or s == 1 else s - 5
                dst = ir[side].at[s - 1, u]
                if half is not None:
                    dst = ir[side].at[s - 1, u, pl.ds(16 * half, 16)]
                i[side, s, u] = remote(
                    term.at[rows(slot(dy, u), half)], dst,
                    i_ss.at[side, s - 1, u], i_rs.at[side, s - 1, u], yn[side],
                )
    ix = remote(xh_s, xh_r, x_ss.at[0], x_rs.at[0], xh)

    def i_step(k):
        s, u = (k + 1) // 2, k % 2
        for side in range(2):
            i[side, s, u].wait_recv()
            if s == 4:
                continue
            dy = 4 - s if side == 0 else s - 4
            if s == 1:
                r = rows(slot(dy, u), side)
                got = ir[side][0, u, pl.ds(16 * side, 16), :]
            else:
                r = rows(slot(dy, u))
                got = ir[side][s - 1, u]
            term[r, :] = (term[r, :].astype(F32) + got.astype(F32)).astype(BF16)
            i[side, s + 1, u].start()
        if s == 4 and u == 1:
            xh_s[...] = (
                term[rows(1), :].astype(F32) + ir_r[3, 1].astype(F32) + ir_l[3, 1].astype(F32)
            ).astype(BF16)
            ix.start()

    cos = [
        remote(w.at[k, :, 1 - core], co_r.at[k], co_ss.at[k], co_rs.at[k], co) for k in range(Z)
    ]

    def w_part(*dzs):
        cols = [
            tok[:, pl.ds(pl.multiple_of(((z + dz + Z) % Z) * 128, 128), 128)] for dz in dzs
        ]
        cols = cols[0] if len(cols) == 1 else jnp.concatenate(cols, axis=1)
        part = lax.dot_general(
            cols, gg[...], (((0,), (0,)), ((), ())), preferred_element_type=F32
        ).astype(BF16)
        for n, dz in enumerate(dzs):
            w[dz % Z] = part[128 * n : 128 * (n + 1)].reshape(2, 2, BLK, part.shape[-1])
            cos[dz % Z].start()

    zrv = (zr_r, zr_l)
    zc = {}
    for side in range(2):
        for k in range(1, 9):
            for q in range(2):
                if k == 8 and q != side:
                    continue
                to = zn2 if k in (7, 5, 3) else zn
                zc[side, k, q] = remote(
                    zs.at[(k if side == 0 else -k) % Z, q], zrv[side].at[k - 1, q],
                    z_ss.at[side, k - 1, q], z_rs.at[side, k - 1, q], to[side],
                )

    def z_send(k):
        for side in range(2):
            if k < 8 or side == 0:
                cos[(k if side == 0 else -k) % Z].wait_recv()
        for q in range(2):
            for side in range(2):
                if k == 8 and q != side:
                    continue
                kk = (k if side == 0 else -k) % Z
                val = w[kk, q, core].astype(F32) + co_r[kk, q].astype(F32)
                if k % 2:
                    for src in (k + 1, k + 2):
                        if (side, src, q) in zc:
                            if src == 8 or src < 8 and (src % 2 == 0 or src in (7, 5, 3)):
                                zc[side, src, q].wait_recv()
                                val = val + zrv[side][src - 1, q].astype(F32)
                zs[kk, q] = val.astype(BF16)
                zc[side, k, q].start()

    w_part(8)
    terms(14, 2)
    for u in (1, 0):
        for side in range(2):
            i[side, 1, u].start()
    w_part(7, -7)
    z_send(8)
    w_part(6, -6)
    w_part(5, -5)
    z_send(6)
    z_send(7)
    w_part(4, -4)
    w_part(3, -3)
    z_send(4)
    i_step(1)
    i_step(2)
    z_send(5)
    w_part(2, -2)
    w_part(1, -1)
    z_send(2)
    i_step(3)
    i_step(4)
    z_send(3)
    w_part(0)
    i_step(5)
    i_step(6)
    z_send(1)
    i_step(7)

    cos[0].wait_recv()
    for q in range(2):
        for side in range(2):
            zc[side, 1, q].wait_recv()

    def total(q):
        return (
            w[0, q, core].astype(F32) + co_r[0, q].astype(F32)
            + zr_r[0, q].astype(F32) + zr_l[0, q].astype(F32)
        )

    xl_s[...] = total(1 - x_lo).astype(BF16)
    xc = remote(xl_s, xl_r, x_ss.at[1], x_rs.at[1], xl)
    xc.start()
    i_step(8)
    mine = total(x_lo)
    xc.wait_recv()
    grad[...] = mine + xl_r[...].astype(F32)
    ix.wait_recv()
    ig[...] = (
        term[rows(0), :].astype(F32) + ir_r[3, 0].astype(F32) + ir_l[3, 0].astype(F32)
        + xh_r[...].astype(F32)
    ).astype(BF16)

    for cp in [xa, *xb.values(), ix, xc, *g.values(), *i.values(), *cos, *zc.values()]:
        cp.wait_send()
    for st in upg_st:
        st.wait()


def finish(ig_in, upg_in, grad_in, m1_in, m2_in, ig, upg, m1, m2, upd):
    grad = grad_in[...] * (1.0 / math.sqrt(32768))
    first = 0.9 * m1_in[...].astype(F32) + 0.1 * grad
    second = 0.95 * m2_in[...].astype(F32) + 0.05 * grad * grad
    upd[...] = first / (jnp.sqrt(second) + 1e-8)
    m1[...] = first.astype(BF16)
    m2[...] = second.astype(BF16)
    ig[...] = ig_in[...]
    upg[...] = upg_in[...]


def local(tokens, gate_weight, up_act, cotangent, moment1, moment2):
    dw, hid = gate_weight.shape
    any_spec = pl.BlockSpec(memory_space=pl.ANY)
    vm_spec = pl.BlockSpec(memory_space=pltpu.VMEM)
    vm = pltpu.VMEM
    dma = pltpu.SemaphoreType.DMA
    upg, ig, grad = pl.pallas_call(
        kernel,
        out_shape=(
            jax.ShapeDtypeStruct((16, BLK, hid), BF16),
            jax.ShapeDtypeStruct((BLK, dw), BF16),
            jax.ShapeDtypeStruct((BLK, hid), F32),
        ),
        in_specs=[any_spec] * 4,
        out_specs=(any_spec, vm_spec, vm_spec),
        scratch_shapes=[
            vm((512, dw), BF16),
            vm((dw, hid), BF16),
            vm((512, hid), BF16),
            vm((512, hid), BF16),
            vm((512, hid), BF16),
            vm((512, hid), BF16),
            vm((512, dw), BF16),
            vm((4, 2, BLK, dw), BF16),
            vm((4, 2, BLK, dw), BF16),
            vm((BLK, dw), BF16),
            vm((BLK, dw), BF16),
            vm((Z, 2, 2, BLK, hid), BF16),
            vm((Z, 2, BLK, hid), BF16),
            vm((Z, 2, BLK, hid), BF16),
            vm((8, 2, BLK, hid), BF16),
            vm((8, 2, BLK, hid), BF16),
            vm((BLK, hid), BF16),
            vm((BLK, hid), BF16),
            dma((2,)), dma((16,)), dma((16,)), dma((16,)),
            dma((2, 4, 3)), dma((2, 4, 3)), dma((9,)), dma((9,)), dma((2,)), dma((2,)),
            dma((Z,)), dma((Z,)), dma((2, 8, 2)), dma((2, 8, 2)),
            dma((2, 4, 2)), dma((2, 4, 2)),
        ],
        compiler_params=pltpu.CompilerParams(collective_id=0, has_side_effects=True),
    )(tokens, gate_weight, up_act.reshape(16, BLK, hid), cotangent.reshape(16, BLK, hid))
    return pl.pallas_call(
        finish,
        out_shape=(
            jax.ShapeDtypeStruct((BLK, dw), BF16),
            jax.ShapeDtypeStruct((512, hid), BF16),
            jax.ShapeDtypeStruct((BLK, hid), BF16),
            jax.ShapeDtypeStruct((BLK, hid), BF16),
            jax.ShapeDtypeStruct((BLK, hid), F32),
        ),
        in_specs=[vm_spec] * 5,
        out_specs=(vm_spec,) * 5,
    )(ig, upg.reshape(512, hid), grad, moment1, moment2)


def solution(mesh):
    rows, cols, both = P(("dp", "tensor"), None), P(None, "tensor"), P("dp", "tensor")
    return jax.shard_map(
        local,
        mesh=mesh,
        in_specs=(rows, cols, both, both, both, both),
        out_specs=(rows, both, both, both, both),
        check_vma=False,
    )
```

time: 88.1 us -> 77.9 us (0.88)
  the two profiles are of different devices: /device:TPU:24 before, /device:TPU:1 now
where the time goes in v2:
time: 77.9 us; the launch traced here: 77.8 us
  Pallas kernels  77.1 us (99%)
    pallas_call x1, Pallas kernels, local(): pl.pallas_call(kernel, out_shape=(jax.ShapeDtypeStruct((16, BLK, hid), BF...  75.1 us
    pallas_call x1, Pallas kernels, local(): pl.pallas_call(finish, out_shape=(jax.ShapeDtypeStruct((BLK, dw), BF16),...  1.99 us

profile of v2, /device:TPU:1, one launch (start us, length us, event | category | flops | bytes accessed | tf_op | source)
XLA Modules:
  0.0 77.8 jit_solution(13342941655082887313)
XLA Ops:
  0.6 75.1 %shard_map.101 = (bf16[16,32,512]{2,1,0:T(8,128)(2,1)}, bf16[32,2048]{1,0:T(8,128)(2,1)}, f32[32,512]{1,0:T(8,128)}) custom-call(bf16[32,2048]{1,0:T(8,128)(2,1)} %tok_in.1, bf16[2048,512]{1,0:T(8,128)(2,1)} %wgt_in.1, bf16[16,32,512]{2,1,0:T(8,128)(2,1)} %bitcast.3, bf16[16,32,512]{2,1,0:T(8,128)(2,1)} %bitcast.4), custom_call_target="tpu_custom_call" | custom-call | tf_op jit(solution)/shard_map/pallas_call | solution.py:328
  75.8 2.0 %shard_map.102 = (bf16[32,2048]{1,0:T(8,128)(2,1)}, bf16[512,512]{1,0:T(8,128)(2,1)}, bf16[32,512]{1,0:T(8,128)(2,1)}, bf16[32,512]{1,0:T(8,128)(2,1)}, f32[32,512]{1,0:T(8,128)}) custom-call(bf16[32,2048]{1,0:T(8,128)(2,1)} %get-tuple-element.8.ig_in, bf16[512,512]{1,0:T(8,128)(2,1)} %bitcast.5, f32[32,512]{1,0:T(8,128)} %get-tuple-element.10.grad_in, ...), custom_call_target="tpu_custom_call" | custom-call | tf_op jit(solution)/shard_map/pallas_call | solution.py:363

commit v3 on v2

--- a/solution.py
+++ b/solution.py
@@ -10,6 +10,7 @@
 F32, BF16 = jnp.float32, jnp.bfloat16
 Y, Z = 8, 16
 BLK = 32
+HOPS = {8: 6, 7: 6, 5: 3, 4: 3, 6: 3, 2: 0, 1: 0, 3: 0}
 
 
 def slot(dy, c):
@@ -26,7 +27,7 @@
     tok, wgt, up, cot, upg, gg, term, ir_r, ir_l, xh_s, xh_r,
     w, co_r, zs, zr_r, zr_l, xl_s, xl_r,
     ld_sem, up_sem, cot_sem, upg_sem,
-    g_ss, g_rs, gx_ss, gx_rs, x_ss, x_rs, co_ss, co_rs, z_ss, z_rs, i_ss, i_rs,
+    g_ss, g_rs, gx_ss, gx_rs, x_ss, x_rs, xc_ss, xc_rs, co_ss, co_rs, z_ss, z_rs, i_ss, i_rs,
 ):
     d = lax.axis_index("dp")
     t = lax.axis_index("tensor")
@@ -34,8 +35,7 @@
     y, x_hi = t // 2, t % 2
     yn = ((d, (t + 2) % 16), (d, (t + 14) % 16))
     xh = (d, t + 1 - 2 * x_hi)
-    zn = (((d + 4) % 64, t), ((d + 60) % 64, t))
-    zn2 = (((d + 8) % 64, t), ((d + 56) % 64, t))
+    zn = {n: (((d + 4 * n) % 64, t), ((d + 64 - 4 * n) % 64, t)) for n in (1, 2, 3)}
     xl = (d + 2 - 4 * x_lo, t)
     co = (d + 1 - 2 * core, t)
 
@@ -69,9 +69,9 @@
         loads[s] = (a, b)
 
     barrier = pltpu.get_barrier_semaphore()
-    for peer in (*yn, xh, *zn, *zn2, xl, co):
+    for peer in (*yn, xh, *zn[1], *zn[2], *zn[3], xl, co):
         pl.semaphore_signal(barrier, inc=1, device_id=peer, device_id_type=pl.DeviceIdType.MESH)
-    pl.semaphore_wait(barrier, 9)
+    pl.semaphore_wait(barrier, 11)
 
     g = {}
     units = ((0, 1), (0, 0), (1, 0))
@@ -178,7 +178,7 @@
                     term.at[rows(slot(dy, u), half)], dst,
                     i_ss.at[side, s - 1, u], i_rs.at[side, s - 1, u], yn[side],
                 )
-    ix = remote(xh_s, xh_r, x_ss.at[0], x_rs.at[0], xh)
+    ix = remote(xh_s, xh_r, x_ss, x_rs, xh)
 
     def i_step(k):
         s, u = (k + 1) // 2, k % 2
@@ -218,34 +218,48 @@
             cos[dz % Z].start()
 
     zrv = (zr_r, zr_l)
+    xc = [remote(xl_s.at[k], xl_r.at[k], xc_ss.at[k], xc_rs.at[k], xl) for k in range(Z)]
     zc = {}
     for side in range(2):
-        for k in range(1, 9):
+        for k, to in HOPS.items():
             for q in range(2):
                 if k == 8 and q != side:
                     continue
-                to = zn2 if k in (7, 5, 3) else zn
                 zc[side, k, q] = remote(
                     zs.at[(k if side == 0 else -k) % Z, q], zrv[side].at[k - 1, q],
-                    z_ss.at[side, k - 1, q], z_rs.at[side, k - 1, q], to[side],
+                    z_ss.at[side, k - 1, q], z_rs.at[side, k - 1, q], zn[k - to][side],
                 )
+
+    def x_send(*dzs):
+        for dz in dzs:
+            k = dz % Z
+            cos[k].wait_recv()
+            xl_s[k] = (
+                w[k, 1 - x_lo, core].astype(F32) + co_r[k, 1 - x_lo].astype(F32)
+            ).astype(BF16)
+            xc[k].start()
+
+    def own(k, q):
+        r = pl.ds(16 * q, 16)
+        return (
+            w[k, x_lo, core, r, :].astype(F32) + co_r[k, x_lo, r, :].astype(F32)
+            + xl_r[k, r, :].astype(F32)
+        )
 
     def z_send(k):
         for side in range(2):
             if k < 8 or side == 0:
-                cos[(k if side == 0 else -k) % Z].wait_recv()
+                xc[(k if side == 0 else -k) % Z].wait_recv()
         for q in range(2):
             for side in range(2):
                 if k == 8 and q != side:
                     continue
                 kk = (k if side == 0 else -k) % Z
-                val = w[kk, q, core].astype(F32) + co_r[kk, q].astype(F32)
-                if k % 2:
-                    for src in (k + 1, k + 2):
-                        if (side, src, q) in zc:
-                            if src == 8 or src < 8 and (src % 2 == 0 or src in (7, 5, 3)):
-                                zc[side, src, q].wait_recv()
-                                val = val + zrv[side][src - 1, q].astype(F32)
+                val = own(kk, q)
+                for src, to in HOPS.items():
+                    if to == k and (side, src, q) in zc:
+                        zc[side, src, q].wait_recv()
+                        val = val + zrv[side][src - 1, q].astype(F32)
                 zs[kk, q] = val.astype(BF16)
                 zc[side, k, q].start()
 
@@ -255,54 +269,54 @@
         for side in range(2):
             i[side, 1, u].start()
     w_part(7, -7)
+    x_send(8)
+    w_part(5, -5)
+    x_send(7, -7)
+    w_part(4, -4)
+    x_send(5, -5)
+    w_part(6, -6)
+    x_send(4, -4)
+    w_part(2, -2)
+    x_send(6, -6)
     z_send(8)
-    w_part(6, -6)
-    w_part(5, -5)
-    z_send(6)
+    w_part(1, -1)
+    x_send(2, -2)
     z_send(7)
-    w_part(4, -4)
+    i_step(1)
     w_part(3, -3)
-    z_send(4)
-    i_step(1)
+    x_send(1, -1)
     i_step(2)
     z_send(5)
-    w_part(2, -2)
-    w_part(1, -1)
+    w_part(0)
+    x_send(3, -3)
+    z_send(4)
+    x_send(0)
+    z_send(6)
+    i_step(3)
     z_send(2)
-    i_step(3)
+    z_send(1)
     i_step(4)
     z_send(3)
-    w_part(0)
     i_step(5)
     i_step(6)
-    z_send(1)
     i_step(7)
 
-    cos[0].wait_recv()
+    xc[0].wait_recv()
     for q in range(2):
-        for side in range(2):
-            zc[side, 1, q].wait_recv()
-
-    def total(q):
-        return (
-            w[0, q, core].astype(F32) + co_r[0, q].astype(F32)
-            + zr_r[0, q].astype(F32) + zr_l[0, q].astype(F32)
-        )
-
-    xl_s[...] = total(1 - x_lo).astype(BF16)
-    xc = remote(xl_s, xl_r, x_ss.at[1], x_rs.at[1], xl)
-    xc.start()
+        val = own(0, q)
+        for k in (1, 2, 3):
+            for side in range(2):
+                zc[side, k, q].wait_recv()
+                val = val + zrv[side][k - 1, q].astype(F32)
+        grad[pl.ds(16 * q, 16), :] = val
     i_step(8)
-    mine = total(x_lo)
-    xc.wait_recv()
-    grad[...] = mine + xl_r[...].astype(F32)
     ix.wait_recv()
     ig[...] = (
         term[rows(0), :].astype(F32) + ir_r[3, 0].astype(F32) + ir_l[3, 0].astype(F32)
         + xh_r[...].astype(F32)
     ).astype(BF16)
 
-    for cp in [xa, *xb.values(), ix, xc, *g.values(), *i.values(), *cos, *zc.values()]:
+    for cp in [xa, *xb.values(), ix, *xc, *g.values(), *i.values(), *cos, *zc.values()]:
         cp.wait_send()
     for st in upg_st:
         st.wait()
@@ -348,13 +362,13 @@
             vm((BLK, dw), BF16),
             vm((Z, 2, 2, BLK, hid), BF16),
             vm((Z, 2, BLK, hid), BF16),
-            vm((Z, 2, BLK, hid), BF16),
-            vm((8, 2, BLK, hid), BF16),
-            vm((8, 2, BLK, hid), BF16),
-            vm((BLK, hid), BF16),
-            vm((BLK, hid), BF16),
+            vm((Z, 2, 16, hid), BF16),
+            vm((8, 2, 16, hid), BF16),
+            vm((8, 2, 16, hid), BF16),
+            vm((Z, BLK, hid), BF16),
+            vm((Z, BLK, hid), BF16),
             dma((2,)), dma((16,)), dma((16,)), dma((16,)),
-            dma((2, 4, 3)), dma((2, 4, 3)), dma((9,)), dma((9,)), dma((2,)), dma((2,)),
+            dma((2, 4, 3)), dma((2, 4, 3)), dma((9,)), dma((9,)), dma, dma, dma((Z,)), dma((Z,)),
             dma((Z,)), dma((Z,)), dma((2, 8, 2)), dma((2, 8, 2)),
             dma((2, 4, 2)), dma((2, 4, 2)),
         ],

time: 77.9 us -> 76.8 us (0.986)
  Pallas kernels: 77.1 us -> 76 us
    pallas_call x1, Pallas kernels: 75.1 us -> 74 us  [local(): pl.pallas_call(kernel, out_shape=(jax.ShapeDtypeStruct((16, BLK, hid), BF...]
where the time goes in v3:
time: 76.8 us; the launch traced here: 76.7 us
  Pallas kernels  76 us (99%)
    pallas_call x1, Pallas kernels, local(): pl.pallas_call(kernel, out_shape=(jax.ShapeDtypeStruct((16, BLK, hid), BF...  74 us
    pallas_call x1, Pallas kernels, local(): pl.pallas_call(finish, out_shape=(jax.ShapeDtypeStruct((BLK, dw), BF16),...  1.99 us

profile of v3, /device:TPU:1, one launch (start us, length us, event | category | flops | bytes accessed | tf_op | source)
XLA Modules:
  0.0 76.7 jit_solution(3163699779780058358)
XLA Ops:
  0.6 74.0 %shard_map.101 = (bf16[16,32,512]{2,1,0:T(8,128)(2,1)}, bf16[32,2048]{1,0:T(8,128)(2,1)}, f32[32,512]{1,0:T(8,128)}) custom-call(bf16[32,2048]{1,0:T(8,128)(2,1)} %tok_in.1, bf16[2048,512]{1,0:T(8,128)(2,1)} %wgt_in.1, bf16[16,32,512]{2,1,0:T(8,128)(2,1)} %bitcast.3, bf16[16,32,512]{2,1,0:T(8,128)(2,1)} %bitcast.4), custom_call_target="tpu_custom_call" | custom-call | tf_op jit(solution)/shard_map/pallas_call | solution.py:342
  74.7 2.0 %shard_map.102 = (bf16[32,2048]{1,0:T(8,128)(2,1)}, bf16[512,512]{1,0:T(8,128)(2,1)}, bf16[32,512]{1,0:T(8,128)(2,1)}, bf16[32,512]{1,0:T(8,128)(2,1)}, f32[32,512]{1,0:T(8,128)}) custom-call(bf16[32,2048]{1,0:T(8,128)(2,1)} %get-tuple-element.8.ig_in, bf16[512,512]{1,0:T(8,128)(2,1)} %bitcast.5, f32[32,512]{1,0:T(8,128)} %get-tuple-element.10.grad_in, ...), custom_call_target="tpu_custom_call" | custom-call | tf_op jit(solution)/shard_map/pallas_call | solution.py:377

commit v4 on v3

--- a/solution.py
+++ b/solution.py
@@ -24,10 +24,10 @@
 def kernel(
     tok_in, wgt_in, up_in, cot_in,
     upg_out, ig, grad,
-    tok, wgt, up, cot, upg, gg, term, ir_r, ir_l, xh_s, xh_r,
+    tok, wgt, up, cot, upg, gg, term, ir_r, ir_l, xh_s, xh_r, pm_r,
     w, co_r, zs, zr_r, zr_l, xl_s, xl_r,
     ld_sem, up_sem, cot_sem, upg_sem,
-    g_ss, g_rs, gx_ss, gx_rs, x_ss, x_rs, xc_ss, xc_rs, co_ss, co_rs, z_ss, z_rs, i_ss, i_rs,
+    g_ss, g_rs, gx_ss, gx_rs, x_ss, x_rs, xc_ss, xc_rs, pm_ss, pm_rs, co_ss, co_rs, z_ss, z_rs, i_ss, i_rs,
 ):
     d = lax.axis_index("dp")
     t = lax.axis_index("tensor")
@@ -95,6 +95,13 @@
         for dy in (0, -1, 1, -2, 2, -3, 3, 4)
     }
 
+    pm = {
+        dy: remote(
+            term.at[rows(slot(dy, 1), int(dy > 0))], pm_r.at[dy + 3],
+            pm_ss.at[dy + 3], pm_rs.at[dy + 3], xh,
+        )
+        for dy in (-1, 1, -2, 2, -3, 3)
+    }
     upg_st = []
 
     def gate(first, count):
@@ -159,6 +166,8 @@
     xb[3].wait_recv()
     gate(10, 4)
     terms(10, 4)
+    pm[3].start()
+    pm[-3].start()
     g[0, 4, 1].wait_recv()
     g[0, 4, 2].wait_recv()
     xb[4].wait_recv()
@@ -169,7 +178,7 @@
     for s in range(1, 5):
         for u in range(2):
             for side in range(2):
-                half = side if s == 1 else None
+                half = side if s == 1 or u == 1 else None
                 dy = 5 - s if side == 0 or s == 1 else s - 5
                 dst = ir[side].at[s - 1, u]
                 if half is not None:
@@ -187,18 +196,25 @@
             if s == 4:
                 continue
             dy = 4 - s if side == 0 else s - 4
-            if s == 1:
-                r = rows(slot(dy, u), side)
-                got = ir[side][0, u, pl.ds(16 * side, 16), :]
-            else:
-                r = rows(slot(dy, u))
-                got = ir[side][s - 1, u]
-            term[r, :] = (term[r, :].astype(F32) + got.astype(F32)).astype(BF16)
+            mine, rest = pl.ds(16 * side, 16), pl.ds(16 - 16 * side, 16)
+            r = rows(slot(dy, u), side)
+            term[r, :] = (
+                term[r, :].astype(F32) + ir[side][s - 1, u, mine, :].astype(F32)
+            ).astype(BF16)
+            if u == 0:
+                r = rows(slot(dy, 0), 1 - side)
+                pm[dy].wait_recv()
+                val = term[r, :].astype(F32) + pm_r[dy + 3].astype(F32)
+                if s > 1:
+                    val = val + ir[side][s - 1, 0, rest, :].astype(F32)
+                term[r, :] = val.astype(BF16)
             i[side, s + 1, u].start()
         if s == 4 and u == 1:
-            xh_s[...] = (
-                term[rows(1), :].astype(F32) + ir_r[3, 1].astype(F32) + ir_l[3, 1].astype(F32)
-            ).astype(BF16)
+            for side in range(2):
+                half = pl.ds(16 * side, 16)
+                xh_s[half, :] = (
+                    term[rows(1, side), :].astype(F32) + ir[side][3, 1, half, :].astype(F32)
+                ).astype(BF16)
             ix.start()
 
     cos = [
@@ -272,12 +288,16 @@
     x_send(8)
     w_part(5, -5)
     x_send(7, -7)
+    pm[2].start()
+    pm[-2].start()
     w_part(4, -4)
     x_send(5, -5)
     w_part(6, -6)
     x_send(4, -4)
     w_part(2, -2)
     x_send(6, -6)
+    pm[1].start()
+    pm[-1].start()
     z_send(8)
     w_part(1, -1)
     x_send(2, -2)
@@ -316,21 +336,37 @@
         + xh_r[...].astype(F32)
     ).astype(BF16)
 
-    for cp in [xa, *xb.values(), ix, *xc, *g.values(), *i.values(), *cos, *zc.values()]:
+    for cp in [xa, *xb.values(), *pm.values(), ix, *xc, *g.values(), *i.values(), *cos, *zc.values()]:
         cp.wait_send()
     for st in upg_st:
         st.wait()
 
 
-def finish(ig_in, upg_in, grad_in, m1_in, m2_in, ig, upg, m1, m2, upd):
-    grad = grad_in[...] * (1.0 / math.sqrt(32768))
-    first = 0.9 * m1_in[...].astype(F32) + 0.1 * grad
-    second = 0.95 * m2_in[...].astype(F32) + 0.05 * grad * grad
+def finish(
+    ig_in, upg_in, grad_in, m1_in, m2_in, ig_out, upg_out, m1_out, m2_out, upd_out,
+    ig, upg, grad_v, m1, m2, nm1, nm2, upd, in_sem, out_sem,
+):
+    ins, bufs = (grad_in, m1_in, m2_in, upg_in, ig_in), (grad_v, m1, m2, upg, ig)
+    gets = [pltpu.make_async_copy(a, b, in_sem.at[n]) for n, (a, b) in enumerate(zip(ins, bufs))]
+    for get in gets:
+        get.start()
+    outs = ((upd, upd_out), (nm1, m1_out), (nm2, m2_out), (upg, upg_out), (ig, ig_out))
+    puts = [pltpu.make_async_copy(a, b, out_sem.at[n]) for n, (a, b) in enumerate(outs)]
+    for n in (0, 1, 2):
+        gets[n].wait()
+    grad = grad_v[...] * (1.0 / math.sqrt(32768))
+    first = 0.9 * m1[...].astype(F32) + 0.1 * grad
+    second = 0.95 * m2[...].astype(F32) + 0.05 * grad * grad
     upd[...] = first / (jnp.sqrt(second) + 1e-8)
-    m1[...] = first.astype(BF16)
-    m2[...] = second.astype(BF16)
-    ig[...] = ig_in[...]
-    upg[...] = upg_in[...]
+    nm1[...] = first.astype(BF16)
+    nm2[...] = second.astype(BF16)
+    for n in (3, 4):
+        gets[n].wait()
+        puts[n].start()
+    for n in (0, 1, 2):
+        puts[n].start()
+    for put in puts:
+        put.wait()
 
 
 def local(tokens, gate_weight, up_act, cotangent, moment1, moment2):
@@ -360,6 +396,7 @@
             vm((4, 2, BLK, dw), BF16),
             vm((BLK, dw), BF16),
             vm((BLK, dw), BF16),
+            vm((7, 16, dw), BF16),
             vm((Z, 2, 2, BLK, hid), BF16),
             vm((Z, 2, BLK, hid), BF16),
             vm((Z, 2, 16, hid), BF16),
@@ -368,7 +405,7 @@
             vm((Z, BLK, hid), BF16),
             vm((Z, BLK, hid), BF16),
             dma((2,)), dma((16,)), dma((16,)), dma((16,)),
-            dma((2, 4, 3)), dma((2, 4, 3)), dma((9,)), dma((9,)), dma, dma, dma((Z,)), dma((Z,)),
+            dma((2, 4, 3)), dma((2, 4, 3)), dma((9,)), dma((9,)), dma, dma, dma((Z,)), dma((Z,)), dma((7,)), dma((7,)),
             dma((Z,)), dma((Z,)), dma((2, 8, 2)), dma((2, 8, 2)),
             dma((2, 4, 2)), dma((2, 4, 2)),
         ],
@@ -383,8 +420,13 @@
             jax.ShapeDtypeStruct((BLK, hid), BF16),
             jax.ShapeDtypeStruct((BLK, hid), F32),
         ),
-        in_specs=[vm_spec] * 5,
-        out_specs=(vm_spec,) * 5,
+        in_specs=[any_spec] * 5,
+        out_specs=(any_spec,) * 5,
+        scratch_shapes=[
+            vm((BLK, dw), BF16), vm((512, hid), BF16), vm((BLK, hid), F32),
+            vm((BLK, hid), BF16), vm((BLK, hid), BF16), vm((BLK, hid), BF16),
+            vm((BLK, hid), BF16), vm((BLK, hid), F32), dma((5,)), dma((5,)),
+        ],
     )(ig, upg.reshape(512, hid), grad, moment1, moment2)
 
 

time: 76.8 us -> 80.1 us (1.043)
  Pallas kernels: 76 us -> 79.3 us
    pallas_call x1, Pallas kernels: 74 us -> 77.2 us  [local(): pl.pallas_call(kernel, out_shape=(jax.ShapeDtypeStruct((16, BLK, hid), BF...]
where the time goes in v4:
time: 80.1 us; the launch traced here: 80 us
  Pallas kernels  79.3 us (99%)
    pallas_call x1, Pallas kernels, local(): pl.pallas_call(kernel, out_shape=(jax.ShapeDtypeStruct((16, BLK, hid), BF...  77.2 us
    pallas_call x1, Pallas kernels, local(): pl.pallas_call(finish, out_shape=(jax.ShapeDtypeStruct((BLK, dw), BF16),...  2.07 us

profile of v4, /device:TPU:1, one launch (start us, length us, event | category | flops | bytes accessed | tf_op | source)
XLA Modules:
  0.0 80.0 jit_solution(4993321840204469418)
XLA Ops:
  0.6 77.2 %shard_map.101 = (bf16[16,32,512]{2,1,0:T(8,128)(2,1)}, bf16[32,2048]{1,0:T(8,128)(2,1)}, f32[32,512]{1,0:T(8,128)}) custom-call(bf16[32,2048]{1,0:T(8,128)(2,1)} %tok_in.1, bf16[2048,512]{1,0:T(8,128)(2,1)} %wgt_in.1, bf16[16,32,512]{2,1,0:T(8,128)(2,1)} %bitcast.3, bf16[16,32,512]{2,1,0:T(8,128)(2,1)} %bitcast.4), custom_call_target="tpu_custom_call" | custom-call | tf_op jit(solution)/shard_map/pallas_call | solution.py:378
  77.9 2.1 %shard_map.102 = (bf16[32,2048]{1,0:T(8,128)(2,1)}, bf16[512,512]{1,0:T(8,128)(2,1)}, bf16[32,512]{1,0:T(8,128)(2,1)}, bf16[32,512]{1,0:T(8,128)(2,1)}, f32[32,512]{1,0:T(8,128)}) custom-call(bf16[32,2048]{1,0:T(8,128)(2,1)} %get-tuple-element.8.ig_in, bf16[512,512]{1,0:T(8,128)(2,1)} %bitcast.5, f32[32,512]{1,0:T(8,128)} %get-tuple-element.10.grad_in, ...), custom_call_target="tpu_custom_call" | custom-call | tf_op jit(solution)/shard_map/pallas_call | solution.py:414

commit v5 on v3

--- a/solution.py
+++ b/solution.py
@@ -264,14 +264,14 @@
                 zc[side, k, q].start()
 
     w_part(8)
+    w_part(7, -7)
     terms(14, 2)
     for u in (1, 0):
         for side in range(2):
             i[side, 1, u].start()
-    w_part(7, -7)
     x_send(8)
+    x_send(7, -7)
     w_part(5, -5)
-    x_send(7, -7)
     w_part(4, -4)
     x_send(5, -5)
     w_part(6, -6)
@@ -279,9 +279,9 @@
     w_part(2, -2)
     x_send(6, -6)
     z_send(8)
+    z_send(7)
     w_part(1, -1)
     x_send(2, -2)
-    z_send(7)
     i_step(1)
     w_part(3, -3)
     x_send(1, -1)

time: 76.8 us -> 76.5 us (level); the launches traced: 76.7 us -> 75.2 us
  Pallas kernels: 76 us -> 74.6 us
    pallas_call x1, Pallas kernels: 74 us -> 72.6 us  [local(): pl.pallas_call(kernel, out_shape=(jax.ShapeDtypeStruct((16, BLK, hid), BF...]
where the time goes in v5:
time: 76.5 us; the launch traced here: 75.2 us
  Pallas kernels  74.6 us (98%)
    pallas_call x1, Pallas kernels, local(): pl.pallas_call(kernel, out_shape=(jax.ShapeDtypeStruct((16, BLK, hid), BF...  72.6 us
    pallas_call x1, Pallas kernels, local(): pl.pallas_call(finish, out_shape=(jax.ShapeDtypeStruct((BLK, dw), BF16),...  1.99 us

profile of v5, /device:TPU:1, one launch (start us, length us, event | category | flops | bytes accessed | tf_op | source)
XLA Modules:
  0.0 75.2 jit_solution(8873202073098458932)
XLA Ops:
  0.6 72.6 %shard_map.101 = (bf16[16,32,512]{2,1,0:T(8,128)(2,1)}, bf16[32,2048]{1,0:T(8,128)(2,1)}, f32[32,512]{1,0:T(8,128)}) custom-call(bf16[32,2048]{1,0:T(8,128)(2,1)} %tok_in.1, bf16[2048,512]{1,0:T(8,128)(2,1)} %wgt_in.1, bf16[16,32,512]{2,1,0:T(8,128)(2,1)} %bitcast.3, bf16[16,32,512]{2,1,0:T(8,128)(2,1)} %bitcast.4), custom_call_target="tpu_custom_call" | custom-call | tf_op jit(solution)/shard_map/pallas_call | solution.py:342
  73.2 2.0 %shard_map.102 = (bf16[32,2048]{1,0:T(8,128)(2,1)}, bf16[512,512]{1,0:T(8,128)(2,1)}, bf16[32,512]{1,0:T(8,128)(2,1)}, bf16[32,512]{1,0:T(8,128)(2,1)}, f32[32,512]{1,0:T(8,128)}) custom-call(bf16[32,2048]{1,0:T(8,128)(2,1)} %get-tuple-element.8.ig_in, bf16[512,512]{1,0:T(8,128)(2,1)} %bitcast.5, f32[32,512]{1,0:T(8,128)} %get-tuple-element.10.grad_in, ...), custom_call_target="tpu_custom_call" | custom-call | tf_op jit(solution)/shard_map/pallas_call | solution.py:377
